TPU v7x, 512 devices: a whole 4x8x8 slice. The times are simulated.
512 devices in a mesh: gx: 64 (over y_lo, z, core), gy: 8 (over x, y_hi).
Axes of the slice: x: 4, y: 8 (y_hi: 2, y_lo: 4; y = y_hi * 4 + y_lo), z: 8, core: 2. Of those that a mesh axis runs over, the one named last changes fastest.
Arguments:
- charge_density: float32 [16, 32, 128, 1024], P(None, None, 'gx', 'gy'), may hold values from -48 to 48
- layer_ids: int32 [32, 128, 1024], P(None, 'gx', 'gy'), may hold values from 0 to 7
- eps_mean: float32 [8], replicated, may hold values from 1 to 4
- eps_fluct: float32 [8, 15], replicated, may hold values from -0.5 to 0.5
- galerkin: float32 [16, 16, 16], replicated, may hold values from -0.5 to 1, as said below
- net_ids: int32 [32, 128, 8], P(None, 'gx', 'gy'), may hold values from 0 to 2047
- net_place: int32 [2048], replicated, may hold values from 0 to 2047, each once
Outputs:
- potential: float32 [16, 32, 128, 1024], P(None, None, 'gx', 'gy')
- charges: float32 [16, 2048], P(None, ('gx', 'gy'))
Inputs may be any that keep to these rules, and one draw needn't show every extreme that they name: `galerkin`: G[0] is the identity; every G[i] is symmetric in j and k; for i >= 1 its diagonal lies within -0.1 to 0.1.
All inputs are finite; a program needn't handle non-finite values.
Results may differ from a plain program's by a relative error of at most 0.0001.
Values sent between devices are 32-bit elements; how exact they have to be, the bound alone decides.
A program may use at most 64 MiB of HBM per device.

v0:
```python
import jax
import jax.numpy as jnp
from jax import lax
from jax.sharding import PartitionSpec as P

charge_scale = 1.0 / 512.0
relax = 0.8


def extended(x, sides, width):
    edges = {}
    for axis, dim in sides:
        size, length = (lax.axis_size(axis), x.shape[dim])
        up = [(i, (i + 1) % size) for i in range(size - 1)]
        last = lax.slice_in_dim(x, length - width, length, axis=dim)
        initial = lax.slice_in_dim(x, 0, width, axis=dim)
        edges[dim] = (
            lax.ppermute(last, axis, up),
            lax.ppermute(initial, axis, [(b, a) for a, b in up]),
        )
    done = []
    for _, dim in sides:
        low, high = edges[dim]
        around = [(width, width) if d in done else (0, 0) for d in range(x.ndim)]
        x = jnp.concatenate([jnp.pad(low, around), x, jnp.pad(high, around)], axis=dim)
        done.append(dim)
    return x


def with_halo(block, sides, width):
    for axis, dim in sides:
        count = lax.axis_size(axis)
        forward = [(i, i + 1) for i in range(count - 1)]
        backward = [(target, source) for source, target in forward]
        low = lax.ppermute(
            lax.slice_in_dim(block, block.shape[dim] - width, None, axis=dim), axis, forward
        )
        high = lax.ppermute(lax.slice_in_dim(block, 0, width, axis=dim), axis, backward)
        block = jnp.concatenate([low, block, high], axis=dim)
    return block


def neighbours(padded):
    centre = padded[:, :, 1:-1, 1:-1]
    total = padded[:, :, 2:, 1:-1] + padded[:, :, :-2, 1:-1]
    total = total + padded[:, :, 1:-1, 2:] + padded[:, :, 1:-1, :-2]
    zpadded = jnp.pad(centre, ((0, 0), (1, 1), (0, 0), (0, 0)))
    return total + zpadded[:, 2:] + zpadded[:, :-2]


def contract(gflat, coeffs, field):
    modes = coeffs.shape[0]
    shape = field.shape
    flat_coeffs = coeffs.reshape(modes, -1)
    flat_field = field.reshape(modes, -1)
    product = (flat_coeffs[:, None, :] * flat_field[None, :, :]).reshape(modes * modes, -1)
    result = jnp.dot(
        gflat, product, precision=lax.Precision.HIGHEST, preferred_element_type=jnp.float32
    )
    return result.reshape(shape)


def permit_from(table, shifted_ids):
    layers = table.shape[1]
    onehot = (
        shifted_ids[None] == jnp.arange(1, layers + 1, dtype=jnp.int32)[:, None, None, None]
    ).astype(jnp.float32)
    flat = jnp.dot(table, onehot.reshape(layers, -1), precision=lax.Precision.HIGHEST)
    return flat.reshape((table.shape[0],) + shifted_ids.shape)


def local(charge_density, layer_ids, eps_mean, eps_fluct, galerkin, net_ids, net_place):
    modes = galerkin.shape[0]
    shape = charge_density.shape
    table = jnp.concatenate([eps_mean[None, :], eps_mean[None, :] * eps_fluct.T], 0)
    shifted_ids = layer_ids + 1
    padded_ids = extended(shifted_ids, (("gx", 1), ("gy", 2)), 1)
    permit_pad = permit_from(table, padded_ids)
    permit = permit_pad[:, :, 1:-1, 1:-1]
    weights = 6.0 * permit + neighbours(permit_pad)
    gdiag = jnp.diagonal(galerkin, axis1=1, axis2=2)
    diag = 0.5 * jnp.dot(
        gdiag.T, weights.reshape(modes, -1), precision=lax.Precision.HIGHEST
    ).reshape(shape)
    gflat = jnp.transpose(galerkin, (2, 0, 1)).reshape(modes, modes * modes)

    def operate(field):
        field_pad = with_halo(field, (("gx", 2), ("gy", 3)), 1)
        weighted_pad = contract(gflat, permit_pad, field_pad)
        near_field = neighbours(field_pad)
        near_weighted = neighbours(weighted_pad)
        return 0.5 * (
            contract(gflat, weights, field) - contract(gflat, permit, near_field) - near_weighted
        )

    potential = relax * charge_density / diag
    potential = potential + relax * (charge_density - operate(potential)) / diag
    flux = operate(potential)
    blocksum = flux.sum(-1).reshape(modes, -1)
    nets = net_place.shape[0]
    block_nets = net_ids.reshape(-1)
    net_table = (block_nets[:, None] == jnp.arange(nets, dtype=jnp.int32)[None, :]).astype(
        jnp.int32
    )
    column = jnp.sum(net_table * net_place[None, :], axis=1)
    placed = (column[:, None] == jnp.arange(nets, dtype=jnp.int32)[None, :]).astype(jnp.float32)
    partial_value = (
        jnp.dot(
            blocksum, placed, precision=lax.Precision.HIGHEST, preferred_element_type=jnp.float32
        )
        * charge_scale
    )
    charges = lax.psum_scatter(partial_value, ("gx", "gy"), scatter_dimension=1, tiled=True)
    return (potential, charges)


def solution(mesh):
    return jax.shard_map(
        local,
        mesh=mesh,
        in_specs=(
            P(None, None, "gx", "gy"),
            P(None, "gx", "gy"),
            P(),
            P(),
            P(),
            P(None, "gx", "gy"),
            P(),
        ),
        out_specs=(P(None, None, "gx", "gy"), P(None, ("gx", "gy"))),
        check_vma=False,
    )
```

profile of v0, /device:TPU:1, one launch (start us, length us, event | category | flops | bytes accessed | tf_op | source)
XLA Modules:
  0.0 476.8 jit_solution(10848918607016395830)
XLA Ops:
  8.1 8.3 %collective-permute-start = (s32[32,2,1]{2,1,0:T(2,128)S(1)}, s32[32,2,1]{2,1,0:T(2,128)S(1)}, u32[]{:S(2)}, u32[]{:S(2)}) collective-permute-start(s32[32,2,1]{2,1,0:T(2,128)S(1)} %get-tuple-element.30), channel_id=1, source_target_pairs={{0,1},{1,2},{2,3},{3,4},{4,5},{5,6},{6,7},{8,9},{9,10},{10,11},{11... | collective-permute-start | bytes 776 | tf_op jit(solution)/shard_map/ppermute | solution.py:18
  17.7 4.8 %collective-permute-start.1 = (s32[32,1,128]{2,1,0:T(1,128)S(1)}, s32[32,1,128]{2,1,0:T(1,128)S(1)}, u32[]{:S(2)}, u32[]{:S(2)}) collective-permute-start(s32[32,1,128]{2,1,0:T(1,128)S(1)} %get-tuple-element.28), channel_id=1, source_target_pairs={{0,8},{8,16},{16,24},{24,32},{32,40},{40,48},{48,56},{56,64},{64,7... | collective-permute-start | bytes 49160 | tf_op jit(solution)/shard_map/ppermute | solution.py:18
  22.5 1.9 collective-permute-start.2
  29.9 3.3 reshape.55
  36.6 1.9 multiply_divide_fusion
  38.5 1.9 collective-permute-start.4
  40.4 3.7 collective-permute-start.5
  48.8 1.8 copy.101
  52.5 9.0 %collective-permute-start.7 = (f32[16,32,4,1]{1,0,3,2:T(8,128)S(1)}, f32[16,32,4,1]{1,0,3,2:T(8,128)S(1)}, u32[]{:S(2)}, u32[]{:S(2)}) collective-permute-start(f32[16,32,4,1]{1,0,3,2:T(8,128)S(1)} %copy.103), channel_id=1, source_target_pairs={{0,1},{1,2},{2,3},{3,4},{4,5},{5,6},{6,7},{8,9},{9,10},{10,11},{11... | collective-permute-start | bytes 24584 | tf_op jit(solution)/shard_map/ppermute | solution.py:35
  61.5 6.5 %convolution_bitcast_fusion.5 = f32[8192,16]{0,1:T(8,128)} fusion(f32[16,8192]{1,0:T(8,128)} %mul.140, f32[16,8192]{1,0:T(8,128)S(1)} %reshape.56, f32[16,16,16]{2,1,0:T(8,128)S(1)} %copy-done.10), kind=kOutput, calls=%fused_computation.12 | convolution fusion | flops 404750336 | bytes 1589248 | tf_op jit(solution)/shard_map/dot_general | solution.py:57
  72.8 2.3 mul.145
  75.1 7.2 %fusion.5 = f32[16,8192]{1,0:T(8,128)} fusion(f32[8192,16]{0,1:T(8,128)} %convolution_bitcast_fusion.5, f32[16,8192]{1,0:T(8,128)} %mul.145, f32[16,8192]{1,0:T(8,128)} %mul.143, f32[16,16,16]{2,1,0:T(8,128)S(1)} %copy-done.10), kind=kOutput, calls=%fused_computation.11 | convolution fusion | flops 404881408 | bytes 2113536 | tf_op jit(solution)/shard_map/dot_general | solution.py:57
  82.3 2.3 sub.29
  86.8 2.5 mul.149
  89.3 11.7 %convolution_bitcast_fusion.1 = f32[16,16640]{1,0:T(8,128)} fusion(f32[16,16640]{1,0:T(8,128)} %mul.149, f32[16,16640]{1,0:T(8,128)S(1)} %copy-done.1, f32[16,16,16]{2,1,0:T(8,128)S(1)} %copy-done.10), kind=kOutput, calls=%fused_computation.2 | convolution fusion | flops 822149120 | bytes 3211264 | tf_op jit(solution)/shard_map/dot_general | solution.py:57
  101.0 4.6 reshape.57
  105.7 2.4 fusion.66
  108.5 1.9 fusion.33
  110.4 1.9 collective-permute-start.8
  112.3 4.7 collective-permute-start.9
  123.3 9.5 %collective-permute-start.11 = (f32[16,32,4,1]{1,0,3,2:T(8,128)S(1)}, f32[16,32,4,1]{1,0,3,2:T(8,128)S(1)}, u32[]{:S(2)}, u32[]{:S(2)}) collective-permute-start(f32[16,32,4,1]{1,0,3,2:T(8,128)S(1)} %copy.122), channel_id=1, source_target_pairs={{0,1},{1,2},{2,3},{3,4},{4,5},{5,6},{6,7},{8,9},{9,10},{10,11},{11... | collective-permute-start | bytes 24584 | tf_op jit(solution)/shard_map/ppermute | solution.py:35
  132.8 6.6 %convolution_bitcast_fusion.3 = f32[8192,16]{0,1:T(8,128)} fusion(f32[16,8192]{1,0:T(8,128)} %mul.154, f32[16,8192]{1,0:T(8,128)} %copy-done.5, f32[16,16,16]{2,1,0:T(8,128)S(1)} %copy-done.10), kind=kOutput, calls=%fused_computation.8 | convolution fusion | flops 404750336 | bytes 1589248 | tf_op jit(solution)/shard_map/dot_general | solution.py:57
  143.0 2.3 mul.157
  145.2 6.9 %fusion.3 = f32[16,8192]{1,0:T(8,128)} fusion(f32[8192,16]{0,1:T(8,128)} %convolution_bitcast_fusion.3, f32[16,8192]{1,0:T(8,128)} %mul.157, f32[16,8192]{1,0:T(8,128)} %mul.143, f32[16,16,16]{2,1,0:T(8,128)S(1)} %copy-done.10), kind=kOutput, calls=%fused_computation.7 | convolution fusion | flops 404881408 | bytes 2113536 | tf_op jit(solution)/shard_map/dot_general | solution.py:57
  152.2 2.3 sub.34
  156.7 2.5 mul.160
  159.2 11.8 %convolution_bitcast_fusion = f32[16,16640]{1,0:T(8,128)} fusion(f32[16,16640]{1,0:T(8,128)} %mul.160, f32[16,16640]{1,0:T(8,128)S(1)} %copy-done.2, f32[16,16,16]{2,1,0:T(8,128)S(1)} %copy-done.10), kind=kOutput, calls=%fused_computation.1 | convolution fusion | flops 822149120 | bytes 3211264 | tf_op jit(solution)/shard_map/dot_general | solution.py:57
  171.0 4.6 reshape.58
  175.6 2.4 fusion.65
  178.3 2.0 fusion.40
  180.4 2.1 convolution_multiply_fusion
  182.5 286.0 %all-reduce.10.cloned.1.call-done = f32[16,2048]{0,1:T(8,128)} async-done(((f32[16,2048]{0,1:T(8,128)}), f32[16,2048]{0,1:T(8,128)}) %all-reduce.10.cloned.1.call-update) | async-done | bytes 131088
  (91 shorter events, 38.5 us)
Async XLA Ops:
  7.2 461.3 %all-reduce.10.cloned.1.call-start = ((), (), s32[]{:S(2)}) async-start(), calls=%async_computation | async-start | bytes 2097152
  8.1 19.5 %collective-permute-start = (s32[32,2,1]{2,1,0:T(2,128)S(1)}, s32[32,2,1]{2,1,0:T(2,128)S(1)}, u32[]{:S(2)}, u32[]{:S(2)}) collective-permute-start(s32[32,2,1]{2,1,0:T(2,128)S(1)} %get-tuple-element.30), channel_id=1, source_target_pairs={{0,1},{1,2},{2,3},{3,4},{4,5},{5,6},{6,7},{8,9},{9,10},{10,11},{11... | collective-permute-start | bytes 776 | tf_op jit(solution)/shard_map/ppermute | solution.py:18
  16.4 11.3 %collective-permute-start.3 = (s32[32,2,1]{2,1,0:T(2,128)S(1)}, s32[32,2,1]{2,1,0:T(2,128)S(1)}, u32[]{:S(2)}, u32[]{:S(2)}) collective-permute-start(s32[32,2,1]{2,1,0:T(2,128)S(1)} %get-tuple-element.31), channel_id=1, source_target_pairs={{1,0},{2,1},{3,2},{4,3},{5,4},{6,5},{7,6},{9,8},{10,9},{11,10},{12... | collective-permute-start | bytes 776 | tf_op jit(solution)/shard_map/ppermute | solution.py:19
  17.7 10.0 %collective-permute-start.1 = (s32[32,1,128]{2,1,0:T(1,128)S(1)}, s32[32,1,128]{2,1,0:T(1,128)S(1)}, u32[]{:S(2)}, u32[]{:S(2)}) collective-permute-start(s32[32,1,128]{2,1,0:T(1,128)S(1)} %get-tuple-element.28), channel_id=1, source_target_pairs={{0,8},{8,16},{16,24},{24,32},{32,40},{40,48},{48,56},{56,64},{64,7... | collective-permute-start | bytes 49160 | tf_op jit(solution)/shard_map/ppermute | solution.py:18
  22.5 5.1 %collective-permute-start.2 = (s32[32,1,128]{2,1,0:T(1,128)S(1)}, s32[32,1,128]{2,1,0:T(1,128)S(1)}, u32[]{:S(2)}, u32[]{:S(2)}) collective-permute-start(s32[32,1,128]{2,1,0:T(1,128)S(1)} %get-tuple-element.29), channel_id=1, source_target_pairs={{8,0},{16,8},{24,16},{32,24},{40,32},{48,40},{56,48},{64,56},{72,6... | collective-permute-start | bytes 49160 | tf_op jit(solution)/shard_map/ppermute | solution.py:19
  28.9 1.0 copy-start
  35.6 1.0 copy-start.7
  36.0 25.5 %copy-start.5 = (f32[16,8192]{1,0:T(8,128)}, f32[16,8192]{1,0:T(8,128)S(1)}, u32[]{:S(2)}) copy-start(f32[16,8192]{1,0:T(8,128)S(1)} %reshape.56) | copy-start | bytes 1572868
  38.5 7.7 %collective-permute-start.4 = (f32[16,32,1,128]{3,0,2,1:T(8,128)S(1)}, f32[16,32,1,128]{3,0,2,1:T(8,128)S(1)}, u32[]{:S(2)}, u32[]{:S(2)}) collective-permute-start(f32[16,32,1,128]{3,0,2,1:T(8,128)S(1)} %get-tuple-element.27), channel_id=1, source_target_pairs={{8,0},{16,8},{24,16},{32,24},{40,32},{48,40},{56,48},{64,56},{72,6... | collective-permute-start | bytes 786440 | tf_op jit(solution)/shard_map/ppermute | solution.py:38
  40.4 7.0 %collective-permute-start.5 = (f32[16,32,1,128]{3,0,2,1:T(8,128)S(1)}, f32[16,32,1,128]{3,0,2,1:T(8,128)S(1)}, u32[]{:S(2)}, u32[]{:S(2)}) collective-permute-start(f32[16,32,1,128]{3,0,2,1:T(8,128)S(1)} %get-tuple-element.26), channel_id=1, source_target_pairs={{0,8},{8,16},{16,24},{24,32},{32,40},{40,48},{48,56},{56,64},{64,7... | collective-permute-start | bytes 786440 | tf_op jit(solution)/shard_map/ppermute | solution.py:35
  48.8 12.7 %copy-start.10 = (f32[16,16,16]{2,1,0:T(8,128)S(1)}, f32[16,16,16]{2,1,0:T(8,128)}, u32[]{:S(2)}) copy-start(f32[16,16,16]{2,1,0:T(8,128)} %param.11) | copy-start | bytes 49156
  50.6 18.6 %collective-permute-start.6 = (f32[16,32,4,1]{1,0,3,2:T(8,128)S(1)}, f32[16,32,4,1]{1,0,3,2:T(8,128)S(1)}, u32[]{:S(2)}, u32[]{:S(2)}) collective-permute-start(f32[16,32,4,1]{1,0,3,2:T(8,128)S(1)} %copy.101), channel_id=1, source_target_pairs={{1,0},{2,1},{3,2},{4,3},{5,4},{6,5},{7,6},{9,8},{10,9},{11,10},{12... | collective-permute-start | bytes 24584 | tf_op jit(solution)/shard_map/ppermute | solution.py:38
  52.5 17.8 %collective-permute-start.7 = (f32[16,32,4,1]{1,0,3,2:T(8,128)S(1)}, f32[16,32,4,1]{1,0,3,2:T(8,128)S(1)}, u32[]{:S(2)}, u32[]{:S(2)}) collective-permute-start(f32[16,32,4,1]{1,0,3,2:T(8,128)S(1)} %copy.103), channel_id=1, source_target_pairs={{0,1},{1,2},{2,3},{3,4},{4,5},{5,6},{6,7},{8,9},{9,10},{10,11},{11... | collective-permute-start | bytes 24584 | tf_op jit(solution)/shard_map/ppermute | solution.py:35
  86.8 2.5 copy-start.1
  105.6 2.8 copy-start.3
  105.6 2.8 copy-start.8
  105.7 2.8 copy-start.9
  108.4 8.6 %copy-start.12 = (s32[32,2,1]{0,2,1:T(1,128)S(1)}, s32[32,2,1]{0,2,1:T(1,128)}, u32[]{:S(2)}) copy-start(s32[32,2,1]{0,2,1:T(1,128)} %param.12) | copy-start | bytes 772
  108.5 8.7 %copy-start.11 = (s32[2048]{0:T(1024)S(1)}, s32[2048]{0:T(1024)}, u32[]{:S(2)}) copy-start(s32[2048]{0:T(1024)} %param.13) | copy-start | bytes 24580
  110.4 8.7 %collective-permute-start.8 = (f32[16,32,1,128]{3,0,2,1:T(8,128)S(1)}, f32[16,32,1,128]{3,0,2,1:T(8,128)S(1)}, u32[]{:S(2)}, u32[]{:S(2)}) collective-permute-start(f32[16,32,1,128]{3,0,2,1:T(8,128)S(1)} %get-tuple-element.25), channel_id=1, source_target_pairs={{8,0},{16,8},{24,16},{32,24},{40,32},{48,40},{56,48},{64,56},{72,6... | collective-permute-start | bytes 786440 | tf_op jit(solution)/shard_map/ppermute | solution.py:38
  112.3 8.0 %collective-permute-start.9 = (f32[16,32,1,128]{3,0,2,1:T(8,128)S(1)}, f32[16,32,1,128]{3,0,2,1:T(8,128)S(1)}, u32[]{:S(2)}, u32[]{:S(2)}) collective-permute-start(f32[16,32,1,128]{3,0,2,1:T(8,128)S(1)} %get-tuple-element.24), channel_id=1, source_target_pairs={{0,8},{8,16},{16,24},{24,32},{32,40},{40,48},{48,56},{56,64},{64,7... | collective-permute-start | bytes 786440 | tf_op jit(solution)/shard_map/ppermute | solution.py:35
  117.7 2.6 copy-start.6
  121.4 18.0 %collective-permute-start.10 = (f32[16,32,4,1]{1,0,3,2:T(8,128)S(1)}, f32[16,32,4,1]{1,0,3,2:T(8,128)S(1)}, u32[]{:S(2)}, u32[]{:S(2)}) collective-permute-start(f32[16,32,4,1]{1,0,3,2:T(8,128)S(1)} %copy.120), channel_id=1, source_target_pairs={{1,0},{2,1},{3,2},{4,3},{5,4},{6,5},{7,6},{9,8},{10,9},{11,10},{12... | collective-permute-start | bytes 24584 | tf_op jit(solution)/shard_map/ppermute | solution.py:38
  123.3 17.1 %collective-permute-start.11 = (f32[16,32,4,1]{1,0,3,2:T(8,128)S(1)}, f32[16,32,4,1]{1,0,3,2:T(8,128)S(1)}, u32[]{:S(2)}, u32[]{:S(2)}) collective-permute-start(f32[16,32,4,1]{1,0,3,2:T(8,128)S(1)} %copy.122), channel_id=1, source_target_pairs={{0,1},{1,2},{2,3},{3,4},{4,5},{5,6},{6,7},{8,9},{9,10},{10,11},{11... | collective-permute-start | bytes 24584 | tf_op jit(solution)/shard_map/ppermute | solution.py:35
  156.7 2.5 copy-start.2
  175.6 2.8 copy-start.4
Sparse Core Ops, SparseCore 0:
  182.6 285.8 all-reduce.9
where the time goes:
time: 486 us; the launch traced here: 477 us
  waiting for transfers between devices  289 us (59%)
  local copies, waits for them, and re-layouts  57.4 us (12%)
  matrix products  55.3 us (11%)
  starting transfers between devices  49.5 us (10%)
  between operations  14.8 us (3%)
  other arithmetic  10.5 us (2%)
    unnamed x2, waiting for transfers between devices  286 us
    dot_general x6, matrix products, contract(): jnp.dot(gflat, product, precision=lax.Precision.HIGHEST, preferred_elemen...  50.7 us
    ppermute x4, starting transfers between devices, with_halo(): lax.ppermute(lax.slice_in_dim(block, block.shape[dim] - width, None, axis...  26.8 us
    mul x7, local copies, waits for them, and re-layouts, contract(): flat_coeffs[:, None, :] * flat_field[None, :, :]  13.2 us
    ppermute x2, starting transfers between devices, extended(): lax.ppermute(last, axis, up)  13.1 us
  transfers between devices with their start and end apart: 13, of which 5 were waited for; matrix products, arithmetic and copies ran while one was open for 5% of the time, Pallas kernels for 0%

commit v1 on v0

v1 whole, which is shorter than its diff:
```python
import functools

import jax
import jax.numpy as jnp
from jax import lax
from jax.experimental import pallas as pl
from jax.experimental.pallas import tpu as pltpu
from jax.sharding import PartitionSpec as P

charge_scale = 1.0 / 512.0
relax = 0.8

Y_LO, SZ, CORES = 4, 8, 2
SX, Y_HI = 4, 2
MODES, LAYERS = 16, 8
NZ, ROWS, LANES = 32, 64, 128
CHUNK = 8
MESH = pl.DeviceIdType.MESH
F32, BF16, I32 = jnp.float32, jnp.bfloat16, jnp.int32

BESIDE = ((-1, 0), (1, 0), (0, -1), (0, 1), (-1, -1), (-1, 1), (1, -1), (1, 1))
SLOT = {offset: q for q, offset in enumerate(BESIDE)}


def lanes(shape):
    return lax.broadcasted_iota(I32, shape, len(shape) - 1)


def rows(shape):
    return lax.broadcasted_iota(I32, shape, 0)


def packed(ids):
    return jnp.where(ids < LAYERS, jnp.left_shift(1, (ids & 7) * 4), 0)


def counts(word):
    out = []
    for l in range(LAYERS):
        one = (lax.shift_right_logical(word, 4 * l) & 15).astype(F32)
        out.append(jnp.concatenate([one, one], 0))
    return out


def wide(ref, r):
    return jnp.broadcast_to(ref[pl.ds(r, 1), :], (8, LANES))


def bits(ids):
    two = jnp.concatenate([ids, ids], 0)
    return [(two & (1 << b)) != 0 for b in range(3)]


def pick(mask, parts):
    for m in mask:
        parts = [jnp.where(m, parts[i + 1], parts[i]) for i in range(0, len(parts), 2)]
    return parts[0]


def weigh(cnt, parts):
    total = cnt[0] * parts[0]
    for c, part in zip(cnt[1:], parts[1:]):
        total = total + c * part
    return total


def apply_all(b3, tiles):
    high = [t.astype(BF16) for t in tiles]
    low = [(t - h.astype(F32)).astype(BF16) for t, h in zip(tiles, high)]
    high = jnp.concatenate(high, 1)
    rhs = jnp.concatenate([high, high, jnp.concatenate(low, 1)], 0)
    u = jnp.dot(b3, rhs, preferred_element_type=F32)
    return [
        [u[l * MODES : (l + 1) * MODES, i * LANES : (i + 1) * LANES] for l in range(LAYERS)]
        for i in range(len(tiles))
    ]


def kernel(
    gx_size, gy_size,
    rho_ref, ids_ref, mean_ref, fluct_ref, g_ref, net_ref, place_ref,
    pot_ref, charge_ref,
    rv, v, w, t, rd, hx, hv, hw, hid, ie, ier, es, er,
    b3_ref, d_ref, idh_ref, cw_ref, chw_ref, c4_ref, oht, s1, r1, s2, r2,
    ie_s, ie_r, hid_s, hid_r, hx_s, hx_r, e_s, e_r, r1_s, r1_r, r2_s, r2_r,
):
    gx, gy = lax.axis_index("gx"), lax.axis_index("gy")
    core, z, y_lo = gx % CORES, (gx // CORES) % SZ, gx // (CORES * SZ)
    x, y_hi = gy // Y_HI, gy % Y_HI
    g1, m_count = SZ * SX, Y_LO * CORES * Y_HI
    group = z * SX + x
    member = (y_lo * CORES + core) * Y_HI + y_hi

    def group_peer(s):
        peer = (group + s) % g1
        return ((y_lo * SZ + peer // SX) * CORES + core, (peer % SX) * Y_HI + y_hi), peer

    def member_peer(s):
        peer = (member + s) % m_count
        lo, c, hi = peer // (CORES * Y_HI), (peer // Y_HI) % CORES, peer % Y_HI
        return ((lo * SZ + z) * CORES + c, x * Y_HI + hi)

    def exists(q):
        dx, dy = BESIDE[q]
        ok = None
        for step, at, size in ((dx, gx, gx_size), (dy, gy, gy_size)):
            if step:
                here = at > 0 if step < 0 else at < size - 1
                ok = here if ok is None else jnp.logical_and(ok, here)
        return ok

    def target(q):
        return (gx + BESIDE[q][0], gy + BESIDE[q][1])

    def back(q):
        return SLOT[(-BESIDE[q][0], -BESIDE[q][1])]

    barrier = pltpu.get_barrier_semaphore()
    expected = g1 - 1 + m_count - 1
    for q in range(8):
        expected = expected + exists(q).astype(I32)

        @pl.when(exists(q))
        def _(q=q):
            pl.semaphore_signal(barrier, inc=1, device_id=target(q), device_id_type=MESH)

    @pl.loop(1, g1)
    def _(s):
        pl.semaphore_signal(barrier, inc=1, device_id=group_peer(s)[0], device_id_type=MESH)

    @pl.loop(1, m_count)
    def _(s):
        pl.semaphore_signal(barrier, inc=1, device_id=member_peer(s), device_id_type=MESH)

    lane16 = lanes((MODES, LANES))
    lane1 = lanes((1, LANES))
    lane64, row64 = lanes((ROWS, LANES)), rows((ROWS, LANES))
    on_low = lane64 == 2 * row64
    on_high = lane64 == ((2 * row64 + 127) & 127)

    own_ids = ids_ref[...]
    ids_f = own_ids.astype(F32)

    def edge_of(low, high):
        both = jnp.where(on_low, low, 0.0) + jnp.where(on_high, high, 0.0)
        return jnp.sum(both, axis=0, keepdims=True).astype(I32)

    net_f = net_ref[...].astype(F32)
    ie[...] = jnp.zeros((8, LANES), I32)
    ie[0:1, :] = edge_of(ids_f[:, 0:1], ids_f[:, 127:128])
    ie[1:2, :] = edge_of(ids_f[:, 1:2], ids_f[:, 126:127])
    ie[2:3, :] = edge_of(net_f, net_f)

    def gather_edge(tile, r, acc):
        mine = jnp.logical_or(lane16 == 2 * r, lane16 == ((2 * r + 127) & 127))
        return jnp.where(mine, pltpu.roll(tile, 2 * r, 1), acc)

    def rearrange(c, acc):
        for i in range(CHUNK):
            r = c * CHUNK + i
            tile = rho_ref[pl.ds(r, MODES, stride=ROWS), :]
            rv[c * (CHUNK // 2) + i // 2, i % 2] = tile
            acc = gather_edge(tile, r, acc)
        return acc

    es[...] = lax.fori_loop(0, ROWS // CHUNK, rearrange, jnp.zeros((MODES, LANES), F32))

    pl.semaphore_wait(barrier, expected)

    def rv_x(q):
        return rv.at[:, q]

    def ie_copy(q):
        return pltpu.make_async_remote_copy(
            ie, ier.at[back(q)], ie_s.at[q], ie_r.at[back(q)], device_id=target(q), device_id_type=MESH
        )

    def hid_copy(q):
        return pltpu.make_async_remote_copy(
            ids_ref, hid.at[back(q)], hid_s.at[q], hid_r.at[back(q)], device_id=target(q), device_id_type=MESH
        )

    def hx_copy(q):
        return pltpu.make_async_remote_copy(
            rv_x(q),
            hx.at[back(q)], hx_s.at[q], hx_r.at[back(q)], device_id=target(q), device_id_type=MESH,
        )

    def e_copy(q):
        return pltpu.make_async_remote_copy(
            es, er.at[back(q) - 2], e_s.at[q - 2], e_r.at[back(q) - 2], device_id=target(q), device_id_type=MESH
        )

    def copies(q):
        found = [ie_copy(q)]
        if q < 2:
            found += [hid_copy(q), hx_copy(q)]
        elif q < 4:
            found += [e_copy(q)]
        return found

    for q in (4, 5, 6, 7, 2, 3, 0, 1):
        @pl.when(exists(q))
        def _(q=q):
            for one in copies(q):
                one.start()

        @pl.when(jnp.logical_not(exists(q)))
        def _(q=q):
            ier[q] = jnp.where(rows((8, LANES)) < 2, LAYERS, -1)
            if q < 2:
                hid[q] = jnp.full((ROWS, LANES), LAYERS, I32)
                hx[q] = jnp.zeros((NZ, MODES, LANES), F32)
            elif q < 4:
                er[q - 2] = jnp.zeros((MODES, LANES), F32)

    for l in range(LAYERS):
        total = g_ref[0]
        for i in range(1, MODES):
            total = total + fluct_ref[l, i - 1] * g_ref[i]
        total = mean_ref[l] * total
        eye = rows((MODES, MODES)) == lanes((MODES, MODES))
        d_ref[l] = jnp.broadcast_to(
            jnp.sum(jnp.where(eye, total, 0.0), axis=1, keepdims=True), (MODES, LANES)
        )
        three = jnp.concatenate([total, total, total], 1)
        high = three.astype(BF16)
        low = (three - high.astype(F32)).astype(BF16).astype(F32)
        at = lanes((MODES, 3 * MODES))
        middle = jnp.logical_and(at >= MODES, at < 2 * MODES)
        b3_ref[pl.ds(l * MODES, MODES), :] = jnp.where(middle, low, high.astype(F32)).astype(BF16)

    zero = jnp.zeros((2, MODES, LANES), F32)
    for ref in (v, w):
        ref[0:2] = zero
        ref[ROWS + 2 : ROWS + 4] = zero

    def wait_recv(q, which):
        @pl.when(exists(q))
        def _():
            pltpu.make_async_remote_copy(
                *which(q), device_id=target(q), device_id_type=MESH
            ).wait_recv()

    for q in range(8):
        wait_recv(q, lambda q: (ie, ier.at[q], ie_s.at[q], ie_r.at[q]))
    for q in range(2):
        wait_recv(q, lambda q: (ids_ref, hid.at[q], hid_s.at[q], hid_r.at[q]))

    even64 = (row64 & 1) == 0
    left, right = hid[0], hid[1]

    def row_swap(low, high):
        return jnp.where(even64, pltpu.roll(low, ROWS - 1, 0), pltpu.roll(high, 1, 0))

    halo_ids = row_swap(left, right)
    outer_ids = jnp.where(even64, left, right)
    idh_ref[...] = halo_ids

    def roll1(row, by):
        return pltpu.roll(jnp.broadcast_to(row, (8, LANES)), by % LANES, 1)[0:1]

    quarter = lane1 & 3

    def beside_row(k):
        from_left, from_right = ier[2][k : k + 1], ier[3][k : k + 1]
        return jnp.where((lane1 & 1) == 0, roll1(from_left, 1), roll1(from_right, -1))

    edge_ids, edge_ids2 = beside_row(0), beside_row(1)
    ll, lr, rl, rr = (ier[q][0:1] for q in (4, 5, 6, 7))
    edge_halo = jnp.where(
        quarter == 0, roll1(ll, -1),
        jnp.where(quarter == 2, roll1(rl, 3), jnp.where(quarter == 3, roll1(lr, -3), roll1(rr, 1))),
    )
    own_edge = ie[0:1, :]

    def to_column(row, mask):
        return jnp.sum(jnp.where(mask, row.astype(F32), 0.0), axis=1, keepdims=True).astype(I32)

    def around_y(p, edge_row):
        word = packed(edge_row)
        low = jnp.bitwise_and(word, 0xFFFF)
        high = lax.shift_right_logical(word, 16)

        def column(mask):
            return to_column(low, mask) + jnp.left_shift(to_column(high, mask), 16)

        below = jnp.where(lane64 == 0, column(on_low), pltpu.roll(p, 1, 1))
        above = jnp.where(lane64 == LANES - 1, column(on_high), pltpu.roll(p, LANES - 1, 1))
        return below + above

    def around_z(p):
        up = jnp.where(row64 < ROWS - 2, pltpu.roll(p, ROWS - 2, 0), 0)
        return up + jnp.where(row64 >= 2, pltpu.roll(p, 2, 0), 0)

    p_own, p_halo = packed(own_ids), packed(halo_ids)
    four = around_z(p_own) + row_swap(p_own, p_own) + p_halo
    c4_ref[...] = four + 4 * p_own
    cw_ref[...] = four + around_y(p_own, edge_ids) + 6 * p_own
    chw_ref[...] = (
        around_z(p_halo) + p_own + packed(outer_ids) + around_y(p_halo, edge_halo) + 6 * p_halo
    )

    edge_z = lax.shift_right_logical((lane1 + 1) & (LANES - 1), 2)
    p_edge = packed(edge_ids)
    edge_low_x = jnp.logical_or(quarter == 0, quarter == 3)
    edge_word = (
        jnp.where(edge_z > 0, roll1(p_edge, 4), 0)
        + jnp.where(edge_z < NZ - 1, roll1(p_edge, -4), 0)
        + jnp.where(edge_low_x, roll1(p_edge, -2), roll1(p_edge, 2))
        + packed(edge_halo) + packed(own_edge) + packed(edge_ids2) + 6 * p_edge
    )

    b3 = b3_ref[...]

    def start(rho, word):
        cnt = counts(word)
        inverse = (2.0 * relax) / weigh(cnt, [d_ref[l] for l in range(LAYERS)])
        return rho * inverse, inverse, cnt

    @pl.loop(0, ROWS // CHUNK)
    def _(c):
        tiles, cnts = [], []
        for i in range(CHUNK):
            r = c * CHUNK + i
            tile, inverse, cnt = start(rv[c * (CHUNK // 2) + i // 2, i % 2], wide(cw_ref, r))
            rd[r] = inverse
            v[r + 2] = tile
            tiles.append(tile)
            cnts.append(cnt)
        u = apply_all(b3, tiles)
        for i in range(CHUNK):
            r = c * CHUNK + i
            w[r + 2] = pick(bits(wide(ids_ref, r)), u[i])
            t[r] = weigh(cnts[i], u[i])

    net_own = ie[2:3, :]
    odd_from = jnp.where(quarter == 3, roll1(ier[0][2:3], -2), roll1(ier[1][2:3], 2))
    nets = (
        jnp.where((lane1 & 1) == 0, net_own, odd_from),
        jnp.where((lane1 & 1) == 0, ier[2][2:3], ier[3][2:3]),
        net_own,
    )
    place = place_ref[...]
    place_parts = jnp.concatenate(
        [lax.shift_right_logical(place, 3).astype(F32), (place & 7).astype(F32)], 0
    ).astype(BF16)
    hi_rows = place.shape[0]
    columns = []
    for net in nets:
        chosen = (rows((LANES, LANES)) == (net & (LANES - 1))).astype(F32).astype(BF16)
        found = jnp.dot(place_parts, chosen, preferred_element_type=F32)
        value = 8.0 * found[:hi_rows] + found[hi_rows:]
        own_row = rows((hi_rows, LANES)) == lax.shift_right_logical(net, 7)
        column = jnp.sum(jnp.where(own_row, value, 0.0), axis=0, keepdims=True)
        columns.append(jnp.where(net < 0, -1.0, column).astype(I32))

    spot = rows((LANES, LANES))
    spot_m, spot_g, spot_c = spot // 8, (spot // 4) & 1, spot & 3
    per_gx = gy_size * 4
    spot_p = (
        ((spot_m // (CORES * Y_HI)) * SZ * CORES + (spot_m // Y_HI) % CORES) * per_gx
        + (spot_g * Y_HI + spot_m % Y_HI) * 4 + spot_c
    )
    spot_p = jnp.where(spot_m < m_count, spot_p, -2)

    @pl.loop(0, g1 // 2)
    def _(pair):
        base = (2 * pair // SX) * CORES * per_gx + ((2 * pair) % SX) * Y_HI * 4
        for b, column in enumerate(columns):
            hit = spot_p == column - base
            hit = jnp.logical_and(hit, spot_p >= 0)
            oht[pl.ds(pl.multiple_of(pair * LANES, LANES), LANES), b * LANES : (b + 1) * LANES] = (
                jnp.where(hit, 1.0, 0.0).astype(BF16)
            )

    for q in range(2):
        wait_recv(q, lambda q: (rv_x(q), hx.at[q], hx_s.at[q], hx_r.at[q]))

    @pl.loop(0, ROWS // CHUNK)
    def _(c):
        tiles = []
        for i in range(CHUNK):
            r = c * CHUNK + i
            tile, _, _ = start(hx[i % 2, c * (CHUNK // 2) + i // 2], wide(chw_ref, r))
            hv[r] = tile
            tiles.append(tile)
        u = apply_all(b3, tiles)
        for i in range(CHUNK):
            r = c * CHUNK + i
            hw[r] = pick(bits(wide(idh_ref, r)), u[i])

    for q in range(2, 4):
        wait_recv(q, lambda q: (es, er.at[q - 2], e_s.at[q - 2], e_r.at[q - 2]))

    even16 = (lane16 & 1) == 0
    edge_rho = jnp.where(even16, pltpu.roll(er[0], 1, 1), pltpu.roll(er[1], LANES - 1, 1))
    edge_v, _, _ = start(edge_rho, jnp.broadcast_to(edge_word, (8, LANES)))
    edge_bits = bits(jnp.broadcast_to(edge_ids, (8, LANES)))
    edge_w = pick(edge_bits, apply_all(b3, [edge_v])[0])

    def beside_y(tile, edge, r):
        mine = pltpu.roll(edge, (LANES - 2 * r) & (LANES - 1), 1)
        below = jnp.where(lane16 == 0, mine, pltpu.roll(tile, 1, 1))
        return below + jnp.where(lane16 == LANES - 1, mine, pltpu.roll(tile, LANES - 1, 1))

    def within(ref, c, i):
        r = c * CHUNK + i
        return ref[r] + ref[r + 4] + ref[c * CHUNK + (i ^ 1) + 2]

    @pl.loop(0, ROWS // CHUNK)
    def _(c):
        tiles = []
        for i in range(CHUNK):
            r = c * CHUNK + i
            tiles.append(within(v, c, i) + hv[r] + beside_y(v[r + 2], edge_v, r))
        u = apply_all(b3, tiles)
        for i in range(CHUNK):
            r = c * CHUNK + i
            near = within(w, c, i) + hw[r] + beside_y(w[r + 2], edge_w, r)
            flux = 0.5 * (t[r] - pick(bits(wide(ids_ref, r)), u[i]) - near)
            result = v[r + 2] + rd[r] * (rv[c * (CHUNK // 2) + i // 2, i % 2] - flux)
            hv[r] = result
            pot_ref[pl.ds(r, MODES, stride=ROWS), :] = result

    @pl.loop(0, ROWS // CHUNK, init_carry=(jnp.zeros((MODES, LANES), F32),) * 2)
    def sums(c, carry):
        acc, edge = carry
        tiles = [hv[c * CHUNK + i] for i in range(CHUNK)]
        u = apply_all(b3, tiles)
        for i in range(CHUNK):
            r = c * CHUNK + i
            v[r + 2] = tiles[i]
            edge = gather_edge(tiles[i], r, edge)
            own = pick(bits(wide(ids_ref, r)), u[i])
            w[r + 2] = own
            t[r] = weigh(counts(wide(c4_ref, r)), u[i])
            out = own + pick(bits(wide(idh_ref, r)), u[i])
            total = -0.5 * jnp.sum(out, axis=1, keepdims=True)
            acc = jnp.where(lane16 == ((2 * r + 127) & 127), total, acc)
        return acc, edge

    acc, edge_p = sums

    @pl.loop(0, ROWS // CHUNK, init_carry=acc)
    def acc(c, acc):
        u = apply_all(b3, [within(v, c, i) for i in range(CHUNK)])
        for i in range(CHUNK):
            r = c * CHUNK + i
            flux = t[r] - pick(bits(wide(ids_ref, r)), u[i]) - within(w, c, i)
            total = 0.5 * jnp.sum(flux, axis=1, keepdims=True)
            acc = jnp.where(lane16 == 2 * r, total, acc)
        return acc

    u = apply_all(b3, [edge_p])[0]
    inside = jnp.broadcast_to(edge_ids, (MODES, LANES)) < LAYERS
    across = 0.5 * (
        pick(bits(jnp.broadcast_to(own_edge, (8, LANES))), u) + jnp.where(inside, pick(edge_bits, u), 0.0)
    )
    blocks = jnp.concatenate([acc, -across, across], 1) * charge_scale
    high = blocks.astype(BF16)
    low = (blocks - high.astype(F32)).astype(BF16)
    parts = jnp.concatenate([high, low], 0)

    alternate = (lanes((8, LANES)) & 4) == 0

    @pl.loop(0, g1 // 2)
    def _(pair):
        placed = lax.dot_general(
            parts, oht[pl.ds(pl.multiple_of(pair * LANES, LANES), LANES), :],
            (((1,), (1,)), ((), ())), preferred_element_type=F32,
        )
        a = placed[0:8] + placed[16:24]
        b = placed[8:16] + placed[24:32]
        s1[2 * pair] = jnp.where(alternate, a, pltpu.roll(b, 4, 1))
        s1[2 * pair + 1] = jnp.where(alternate, pltpu.roll(a, LANES - 4, 1), b)

    def r1_copy(s):
        device, peer = group_peer(s)
        return pltpu.make_async_remote_copy(
            s1.at[peer], r1.at[s], r1_s.at[s], r1_r.at[s], device_id=device, device_id_type=MESH
        )

    def r2_copy(s):
        return pltpu.make_async_remote_copy(
            s2, r2.at[s], r2_s.at[s], r2_r.at[s], device_id=member_peer(s), device_id_type=MESH
        )

    @pl.loop(1, g1)
    def _(s):
        r1_copy(s).start()

    @pl.loop(1, g1, init_carry=s1[group])
    def share(s, total):
        r1_copy(s).wait_recv()
        return total + r1[s]

    s2[...] = share

    @pl.loop(1, m_count)
    def _(s):
        r2_copy(s).start()

    @pl.loop(1, m_count, init_carry=share)
    def final(s, total):
        r2_copy(s).wait_recv()
        return total + r2[s]

    turned = pltpu.roll(final, (LANES - 8 * member) & (LANES - 1), 1)
    charge_ref[...] = turned

    @pl.loop(1, g1)
    def _(s):
        r1_copy(s).wait_send()

    @pl.loop(1, m_count)
    def _(s):
        r2_copy(s).wait_send()

    for q in range(8):
        @pl.when(exists(q))
        def _(q=q):
            for one in copies(q):
                one.wait_send()


def local(gx_size, gy_size, charge_density, layer_ids, eps_mean, eps_fluct, galerkin, net_ids, net_place):
    vmem = pl.BlockSpec(memory_space=pltpu.VMEM)
    smem = pl.BlockSpec(memory_space=pltpu.SMEM)
    g1, m_count = SZ * SX, Y_LO * CORES * Y_HI
    tile = (MODES, LANES)
    dma = pltpu.SemaphoreType.DMA
    potential, charges = pl.pallas_call(
        functools.partial(kernel, gx_size, gy_size),
        out_shape=(
            jax.ShapeDtypeStruct((MODES * ROWS, LANES), F32),
            jax.ShapeDtypeStruct((8, LANES), F32),
        ),
        in_specs=[vmem, vmem, smem, smem, vmem, vmem, vmem],
        out_specs=(vmem, vmem),
        scratch_shapes=[
            pltpu.VMEM((NZ, 2) + tile, F32),
            pltpu.VMEM((ROWS + 4,) + tile, F32),
            pltpu.VMEM((ROWS + 4,) + tile, F32),
            pltpu.VMEM((ROWS,) + tile, F32),
            pltpu.VMEM((ROWS,) + tile, F32),
            pltpu.VMEM((2, NZ) + tile, F32),
            pltpu.VMEM((ROWS,) + tile, F32),
            pltpu.VMEM((ROWS,) + tile, F32),
            pltpu.VMEM((2, ROWS, LANES), I32),
            pltpu.VMEM((8, LANES), I32),
            pltpu.VMEM((8, 8, LANES), I32),
            pltpu.VMEM(tile, F32),
            pltpu.VMEM((2,) + tile, F32),
            pltpu.VMEM((LAYERS * MODES, 3 * MODES), BF16),
            pltpu.VMEM((LAYERS,) + tile, F32),
            pltpu.VMEM((ROWS, LANES), I32),
            pltpu.VMEM((ROWS, LANES), I32),
            pltpu.VMEM((ROWS, LANES), I32),
            pltpu.VMEM((ROWS, LANES), I32),
            pltpu.VMEM((g1 // 2 * LANES, 3 * LANES), BF16),
            pltpu.VMEM((g1, 8, LANES), F32),
            pltpu.VMEM((g1, 8, LANES), F32),
            pltpu.VMEM((8, LANES), F32),
            pltpu.VMEM((m_count, 8, LANES), F32),
            dma((8,)), dma((8,)), dma((2,)), dma((2,)), dma((2,)), dma((2,)), dma((2,)), dma((2,)),
            dma((g1,)), dma((g1,)), dma((m_count,)), dma((m_count,)),
        ],
        compiler_params=pltpu.CompilerParams(
            collective_id=0, has_side_effects=True, vmem_limit_bytes=48 * 1024 * 1024
        ),
    )(
        charge_density.reshape(MODES * ROWS, LANES),
        layer_ids.reshape(ROWS, LANES),
        eps_mean,
        eps_fluct,
        galerkin,
        net_ids.reshape(ROWS, 1),
        net_place.reshape(-1, LANES),
    )
    mine = charges[:, :8].reshape(8, 2, 4)
    charges = jnp.transpose(mine, (1, 0, 2)).reshape(MODES, 4)
    return potential.reshape(charge_density.shape), charges


def solution(mesh):
    return jax.shard_map(
        functools.partial(local, mesh.shape["gx"], mesh.shape["gy"]),
        mesh=mesh,
        in_specs=(
            P(None, None, "gx", "gy"),
            P(None, "gx", "gy"),
            P(),
            P(),
            P(),
            P(None, "gx", "gy"),
            P(),
        ),
        out_specs=(P(None, None, "gx", "gy"), P(None, ("gx", "gy"))),
        check_vma=False,
    )
```

time: 486 us -> 58.6 us (0.12); the launches traced: 477 us -> 58.3 us
  waiting for transfers between devices: 289 us -> 0 us
  matrix products: 55.3 us -> 0 us
  Pallas kernels: 0 us -> 52.7 us
  local copies, waits for them, and re-layouts: 57.4 us -> 4.94 us
  starting transfers between devices: 49.5 us -> 0 us
  between operations: 14.8 us -> 0.66 us
  other arithmetic: 10.5 us -> 0 us
    unnamed x2 -> x0, waiting for transfers between devices: 286 us -> none
    dot_general x9 -> x0, matrix products: 55.3 us -> none  [the longest x6 50.7 us: contract(): jnp.dot(gflat, product, precision=lax.Precision.HIGHEST, preferred_elemen...]
    pallas_call x0 -> x1, Pallas kernels: none -> 52.7 us  [local(): pl.pallas_call(functools.partial(kernel, gx_size, gy_size), out_shape=(ja...]
    ppermute x12 -> x0, starting transfers between devices: 49.5 us -> none  [the longest x4 26.8 us: with_halo(): lax.ppermute(lax.slice_in_dim(block, block.shape[dim] - width, None, axis...]
    mul x7 -> x0, local copies, waits for them, and re-layouts: 13.2 us -> none  [contract(): flat_coeffs[:, None, :] * flat_field[None, :, :]]
    reshape x4 -> x2, local copies, waits for them, and re-layouts: 12.9 us -> 0.73 us  [the longest x1 0.66 us: local(): charges = jnp.transpose(mine, (1, 0, 2)).reshape(MODES, 4)]
    slice x13 -> x1, local copies, waits for them, and re-layouts: 11 us -> 0.07 us  [local(): mine = charges[:, :8].reshape(8, 2, 4)]
    add x6 -> x0, other arithmetic: 5.29 us -> none  [the longest x1 1.88 us: local(): potential = potential + relax * (charge_density - operate(potential)) / diag]
  transfers between devices with their start and end apart: 13 -> 0, of which waited for: 5 -> 0; matrix products, arithmetic and copies ran while one was open for 5% -> 0% of each run, Pallas kernels for 0% -> 0%
where the time goes in v1:
time: 58.6 us; the launch traced here: 58.3 us
  Pallas kernels  52.7 us (90%)
  local copies, waits for them, and re-layouts  4.94 us (8%)
  between operations  0.66 us (1%)
    pallas_call x1, Pallas kernels, local(): pl.pallas_call(functools.partial(kernel, gx_size, gy_size), out_shape=(ja...  52.7 us
    unnamed x16, local copies, waits for them, and re-layouts  4.13 us

profile of v1, /device:TPU:1, one launch (start us, length us, event | category | flops | bytes accessed | tf_op | source)
XLA Modules:
  0.0 58.3 jit_solution(1963190272605347223)
XLA Ops:
  0.6 0.0 copy-start.6
  0.6 0.7 %copy-done.6 = s32[32,2,1]{0,2,1:T(1,128)S(1)} copy-done((s32[32,2,1]{0,2,1:T(1,128)S(1)}, s32[32,2,1]{0,2,1:T(1,128)}, u32[]{:S(2)}) %copy-start.6) | copy-done | bytes 280
  1.3 0.0 copy-start.2
  1.3 0.1 copy.13
  1.4 0.0 copy-start.3
  1.4 0.0 copy-start.4
  1.4 0.0 copy-start.5
  1.4 0.1 reshape.32.net_ref
  1.5 0.6 %copy-done.2 = s32[32,2,128]{2,1,0:T(2,128)S(1)} copy-done((s32[32,2,128]{2,1,0:T(2,128)S(1)}, s32[32,2,128]{2,1,0:T(2,128)}, u32[]{:S(2)}) %copy-start.2) | copy-done | bytes 32792
  2.1 0.0 copy-done.3
  2.1 0.0 copy-done.4
  2.1 0.0 copy-done.5
  2.1 0.0 copy-start
  2.1 1.0 %copy-done = f32[16,32,2,128]{3,2,1,0:T(2,128)S(1)} copy-done((f32[16,32,2,128]{3,2,1,0:T(2,128)S(1)}, f32[16,32,2,128]{3,2,1,0:T(2,128)}, u32[]{:S(2)}) %copy-start) | copy-done | bytes 524312
  3.2 0.0 copy-start.1
  3.2 0.9 %copy-done.1 = f32[16,16,16]{2,1,0:T(8,128)S(1)} copy-done((f32[16,16,16]{2,1,0:T(8,128)S(1)}, f32[16,16,16]{2,1,0:T(8,128)}, u32[]{:S(2)}) %copy-start.1) | copy-done | bytes 16408
  4.1 52.7 %shard_map.86 = (f32[1024,128]{1,0:T(8,128)S(1)}, f32[8,128]{1,0:T(8,128)S(1)}) custom-call(f32[1024,128]{1,0:T(8,128)S(1)} %bitcast.12, s32[64,128]{1,0:T(8,128)S(1)} %bitcast.14, f32[8]{0:T(128)S(1)} %copy-done.5, f32[8,15]{1,0:T(8,128)S(1)} %copy-done.4, f32[16,16,16]{2,1,0:T(8,128)S(1)} %copy-done.1, s32[64,1]{1,0:T(8,128)S(1)} %reshape.32.net_ref, ...), custom_call_target="tpu_custom_call" | custom-call | tf_op jit(solution)/shard_map/pallas_call | solution.py:533
  56.8 0.1 copy.15
  56.9 0.7 %reshape.31 = f32[16,4]{0,1:T(4,128)} reshape(f32[2,8,4]{1,0,2:T(2,128)S(1)} %copy.16) | data formatting | bytes 512 | tf_op jit(solution)/shard_map/reshape | solution.py:582
  57.5 0.8 %copy.18 = f32[16,32,2,128]{3,2,1,0:T(2,128)} copy(f32[16,32,2,128]{3,2,1,0:T(2,128)S(1)} %bitcast.13) | data formatting | bytes 1048576
  (1 shorter events, 0.0 us)
Async XLA Ops:
  0.6 0.7 %copy-start.6 = (s32[32,2,1]{0,2,1:T(1,128)S(1)}, s32[32,2,1]{0,2,1:T(1,128)}, u32[]{:S(2)}) copy-start(s32[32,2,1]{0,2,1:T(1,128)} %param.12) | copy-start | bytes 772
  1.3 0.8 %copy-start.2 = (s32[32,2,128]{2,1,0:T(2,128)S(1)}, s32[32,2,128]{2,1,0:T(2,128)}, u32[]{:S(2)}) copy-start(s32[32,2,128]{2,1,0:T(2,128)} %param.8) | copy-start | bytes 98308
  1.4 0.7 %copy-start.3 = (s32[2048]{0:T(1024)S(1)}, s32[2048]{0:T(1024)}, u32[]{:S(2)}) copy-start(s32[2048]{0:T(1024)} %param.13) | copy-start | bytes 24580
  1.4 0.7 %copy-start.4 = (f32[8,15]{1,0:T(8,128)S(1)}, f32[8,15]{1,0:T(8,128)}, u32[]{:S(2)}) copy-start(f32[8,15]{1,0:T(8,128)} %fluct_ref.1) | copy-start | bytes 1444
  1.4 0.7 %copy-start.5 = (f32[8]{0:T(128)S(1)}, f32[8]{0:T(128)}, u32[]{:S(2)}) copy-start(f32[8]{0:T(128)} %mean_ref.1) | copy-start | bytes 100
  2.1 1.0 %copy-start = (f32[16,32,2,128]{3,2,1,0:T(2,128)S(1)}, f32[16,32,2,128]{3,2,1,0:T(2,128)}, u32[]{:S(2)}) copy-start(f32[16,32,2,128]{3,2,1,0:T(2,128)} %param.7) | copy-start | bytes 1572868
  3.2 0.9 %copy-start.1 = (f32[16,16,16]{2,1,0:T(8,128)S(1)}, f32[16,16,16]{2,1,0:T(8,128)}, u32[]{:S(2)}) copy-start(f32[16,16,16]{2,1,0:T(8,128)} %g_ref.1) | copy-start | bytes 49156

commit v2 on v1

--- a/solution.py
+++ b/solution.py
@@ -78,8 +78,10 @@
 
 def kernel(
     gx_size, gy_size,
-    rho_ref, ids_ref, mean_ref, fluct_ref, g_ref, net_ref, place_ref,
-    pot_ref, charge_ref,
+    rho_hbm, ids_hbm, mean_hbm, fluct_hbm, g_hbm, net_hbm, place_hbm,
+    pot_hbm, charge_ref,
+    pot_ref, pot_s,
+    rho_ref, ids_ref, mean_ref, fluct_ref, g_ref, net_ref, place_ref, in_s,
     rv, v, w, t, rd, hx, hv, hw, hid, ie, ier, es, er,
     b3_ref, d_ref, idh_ref, cw_ref, chw_ref, c4_ref, oht, s1, r1, s2, r2,
     ie_s, ie_r, hid_s, hid_r, hx_s, hx_r, e_s, e_r, r1_s, r1_r, r2_s, r2_r,
@@ -115,6 +117,16 @@
     def back(q):
         return SLOT[(-BESIDE[q][0], -BESIDE[q][1])]
 
+    fetch = [
+        pltpu.make_async_copy(source, here, in_s.at[i])
+        for i, (source, here) in enumerate((
+            (rho_hbm, rho_ref), (ids_hbm, ids_ref), (net_hbm, net_ref), (g_hbm, g_ref),
+            (fluct_hbm, fluct_ref), (mean_hbm, mean_ref), (place_hbm, place_ref),
+        ))
+    ]
+    for one in fetch:
+        one.start()
+
     barrier = pltpu.get_barrier_semaphore()
     expected = g1 - 1 + m_count - 1
     for q in range(8):
@@ -138,6 +150,8 @@
     on_low = lane64 == 2 * row64
     on_high = lane64 == ((2 * row64 + 127) & 127)
 
+    fetch[1].wait()
+    fetch[2].wait()
     own_ids = ids_ref[...]
     ids_f = own_ids.astype(F32)
 
@@ -145,11 +159,21 @@
         both = jnp.where(on_low, low, 0.0) + jnp.where(on_high, high, 0.0)
         return jnp.sum(both, axis=0, keepdims=True).astype(I32)
 
-    net_f = net_ref[...].astype(F32)
-    ie[...] = jnp.zeros((8, LANES), I32)
-    ie[0:1, :] = edge_of(ids_f[:, 0:1], ids_f[:, 127:128])
-    ie[1:2, :] = edge_of(ids_f[:, 1:2], ids_f[:, 126:127])
-    ie[2:3, :] = edge_of(net_f, net_f)
+    net_own = jnp.zeros((1, LANES), F32)
+    for x_row in range(2):
+        net = jnp.broadcast_to(net_ref[x_row], (8, NZ))
+        wanted = 4 * rows((NZ, LANES)) + 2 * x_row
+        spread = jnp.logical_or(
+            lanes((NZ, LANES)) == wanted, lanes((NZ, LANES)) == ((wanted + 127) & 127)
+        ).astype(F32).astype(BF16)
+        for part, scale in ((lax.shift_right_logical(net, 3), 8.0), (net & 7, 1.0)):
+            part = part.astype(F32).astype(BF16)
+            net_own = net_own + scale * jnp.dot(part, spread, preferred_element_type=F32)[0:1]
+    net_own = net_own.astype(I32)
+    own_edge = edge_of(ids_f[:, 0:1], ids_f[:, 127:128])
+    ie[0] = own_edge
+    ie[1] = edge_of(ids_f[:, 1:2], ids_f[:, 126:127])
+    ie[2] = net_own
 
     def gather_edge(tile, r, acc):
         mine = jnp.logical_or(lane16 == 2 * r, lane16 == ((2 * r + 127) & 127))
@@ -163,6 +187,7 @@
             acc = gather_edge(tile, r, acc)
         return acc
 
+    fetch[0].wait()
     es[...] = lax.fori_loop(0, ROWS // CHUNK, rearrange, jnp.zeros((MODES, LANES), F32))
 
     pl.semaphore_wait(barrier, expected)
@@ -170,9 +195,12 @@
     def rv_x(q):
         return rv.at[:, q]
 
+    def ie_part(ref, q):
+        return ref.at[2] if q < 2 else ref if q < 4 else ref.at[0]
+
     def ie_copy(q):
         return pltpu.make_async_remote_copy(
-            ie, ier.at[back(q)], ie_s.at[q], ie_r.at[back(q)], device_id=target(q), device_id_type=MESH
+            ie_part(ie, q), ie_part(ier.at[back(q)], q), ie_s.at[q], ie_r.at[back(q)], device_id=target(q), device_id_type=MESH
         )
 
     def hid_copy(q):
@@ -207,13 +235,17 @@
 
         @pl.when(jnp.logical_not(exists(q)))
         def _(q=q):
-            ier[q] = jnp.where(rows((8, LANES)) < 2, LAYERS, -1)
+            for k in (0, 1):
+                ier[q, k] = jnp.full((1, LANES), LAYERS, I32)
+            ier[q, 2] = jnp.full((1, LANES), -1, I32)
             if q < 2:
                 hid[q] = jnp.full((ROWS, LANES), LAYERS, I32)
                 hx[q] = jnp.zeros((NZ, MODES, LANES), F32)
             elif q < 4:
                 er[q - 2] = jnp.zeros((MODES, LANES), F32)
 
+    for one in fetch[3:6]:
+        one.wait()
     for l in range(LAYERS):
         total = g_ref[0]
         for i in range(1, MODES):
@@ -242,8 +274,11 @@
                 *which(q), device_id=target(q), device_id_type=MESH
             ).wait_recv()
 
-    for q in range(8):
-        wait_recv(q, lambda q: (ie, ier.at[q], ie_s.at[q], ie_r.at[q]))
+    def wait_ie(q):
+        wait_recv(q, lambda q: (ie_part(ie, q), ie_part(ier.at[q], q), ie_s.at[q], ie_r.at[q]))
+
+    for q in range(4):
+        wait_ie(q)
     for q in range(2):
         wait_recv(q, lambda q: (ids_ref, hid.at[q], hid_s.at[q], hid_r.at[q]))
 
@@ -263,16 +298,10 @@
     quarter = lane1 & 3
 
     def beside_row(k):
-        from_left, from_right = ier[2][k : k + 1], ier[3][k : k + 1]
+        from_left, from_right = ier[2, k], ier[3, k]
         return jnp.where((lane1 & 1) == 0, roll1(from_left, 1), roll1(from_right, -1))
 
     edge_ids, edge_ids2 = beside_row(0), beside_row(1)
-    ll, lr, rl, rr = (ier[q][0:1] for q in (4, 5, 6, 7))
-    edge_halo = jnp.where(
-        quarter == 0, roll1(ll, -1),
-        jnp.where(quarter == 2, roll1(rl, 3), jnp.where(quarter == 3, roll1(lr, -3), roll1(rr, 1))),
-    )
-    own_edge = ie[0:1, :]
 
     def to_column(row, mask):
         return jnp.sum(jnp.where(mask, row.astype(F32), 0.0), axis=1, keepdims=True).astype(I32)
@@ -297,20 +326,6 @@
     four = around_z(p_own) + row_swap(p_own, p_own) + p_halo
     c4_ref[...] = four + 4 * p_own
     cw_ref[...] = four + around_y(p_own, edge_ids) + 6 * p_own
-    chw_ref[...] = (
-        around_z(p_halo) + p_own + packed(outer_ids) + around_y(p_halo, edge_halo) + 6 * p_halo
-    )
-
-    edge_z = lax.shift_right_logical((lane1 + 1) & (LANES - 1), 2)
-    p_edge = packed(edge_ids)
-    edge_low_x = jnp.logical_or(quarter == 0, quarter == 3)
-    edge_word = (
-        jnp.where(edge_z > 0, roll1(p_edge, 4), 0)
-        + jnp.where(edge_z < NZ - 1, roll1(p_edge, -4), 0)
-        + jnp.where(edge_low_x, roll1(p_edge, -2), roll1(p_edge, 2))
-        + packed(edge_halo) + packed(own_edge) + packed(edge_ids2) + 6 * p_edge
-    )
-
     b3 = b3_ref[...]
 
     def start(rho, word):
@@ -334,11 +349,11 @@
             w[r + 2] = pick(bits(wide(ids_ref, r)), u[i])
             t[r] = weigh(cnts[i], u[i])
 
-    net_own = ie[2:3, :]
-    odd_from = jnp.where(quarter == 3, roll1(ier[0][2:3], -2), roll1(ier[1][2:3], 2))
+    fetch[6].wait()
+    odd_from = jnp.where(quarter == 3, roll1(ier[0, 2], -2), roll1(ier[1, 2], 2))
     nets = (
         jnp.where((lane1 & 1) == 0, net_own, odd_from),
-        jnp.where((lane1 & 1) == 0, ier[2][2:3], ier[3][2:3]),
+        jnp.where((lane1 & 1) == 0, ier[2, 2], ier[3, 2]),
         net_own,
     )
     place = place_ref[...]
@@ -374,6 +389,27 @@
                 jnp.where(hit, 1.0, 0.0).astype(BF16)
             )
 
+    for q in range(4, 8):
+        wait_ie(q)
+    ll, lr, rl, rr = (ier[q, 0] for q in (4, 5, 6, 7))
+    edge_halo = jnp.where(
+        quarter == 0, roll1(ll, -1),
+        jnp.where(quarter == 2, roll1(rl, 3), jnp.where(quarter == 3, roll1(lr, -3), roll1(rr, 1))),
+    )
+    chw_ref[...] = (
+        around_z(p_halo) + p_own + packed(outer_ids) + around_y(p_halo, edge_halo) + 6 * p_halo
+    )
+
+    edge_z = lax.shift_right_logical((lane1 + 1) & (LANES - 1), 2)
+    p_edge = packed(edge_ids)
+    edge_low_x = jnp.logical_or(quarter == 0, quarter == 3)
+    edge_word = (
+        jnp.where(edge_z > 0, roll1(p_edge, 4), 0)
+        + jnp.where(edge_z < NZ - 1, roll1(p_edge, -4), 0)
+        + jnp.where(edge_low_x, roll1(p_edge, -2), roll1(p_edge, 2))
+        + packed(edge_halo) + packed(own_edge) + packed(edge_ids2) + 6 * p_edge
+    )
+
     for q in range(2):
         wait_recv(q, lambda q: (rv_x(q), hx.at[q], hx_s.at[q], hx_r.at[q]))
 
@@ -422,6 +458,9 @@
             result = v[r + 2] + rd[r] * (rv[c * (CHUNK // 2) + i // 2, i % 2] - flux)
             hv[r] = result
             pot_ref[pl.ds(r, MODES, stride=ROWS), :] = result
+
+    put = pltpu.make_async_copy(pot_ref, pot_hbm, pot_s)
+    put.start()
 
     @pl.loop(0, ROWS // CHUNK, init_carry=(jnp.zeros((MODES, LANES), F32),) * 2)
     def sums(c, carry):
@@ -464,14 +503,13 @@
 
     alternate = (lanes((8, LANES)) & 4) == 0
 
-    @pl.loop(0, g1 // 2)
-    def _(pair):
-        placed = lax.dot_general(
-            parts, oht[pl.ds(pl.multiple_of(pair * LANES, LANES), LANES), :],
-            (((1,), (1,)), ((), ())), preferred_element_type=F32,
-        )
-        a = placed[0:8] + placed[16:24]
-        b = placed[8:16] + placed[24:32]
+    placed = lax.dot_general(
+        parts, oht[...], (((1,), (1,)), ((), ())), preferred_element_type=F32
+    )
+    placed = placed[:MODES] + placed[MODES:]
+    for pair in range(g1 // 2):
+        a = placed[0:8, pair * LANES : (pair + 1) * LANES]
+        b = placed[8:16, pair * LANES : (pair + 1) * LANES]
         s1[2 * pair] = jnp.where(alternate, a, pltpu.roll(b, 4, 1))
         s1[2 * pair + 1] = jnp.where(alternate, pltpu.roll(a, LANES - 4, 1), b)
 
@@ -507,7 +545,8 @@
         return total + r2[s]
 
     turned = pltpu.roll(final, (LANES - 8 * member) & (LANES - 1), 1)
-    charge_ref[...] = turned
+    turned = turned.T
+    charge_ref[...] = jnp.concatenate([turned[0:4], turned[4:8]], 1)
 
     @pl.loop(1, g1)
     def _(s):
@@ -523,10 +562,12 @@
             for one in copies(q):
                 one.wait_send()
 
+    put.wait()
+
 
 def local(gx_size, gy_size, charge_density, layer_ids, eps_mean, eps_fluct, galerkin, net_ids, net_place):
     vmem = pl.BlockSpec(memory_space=pltpu.VMEM)
-    smem = pl.BlockSpec(memory_space=pltpu.SMEM)
+    hbm = pl.BlockSpec(memory_space=pltpu.HBM)
     g1, m_count = SZ * SX, Y_LO * CORES * Y_HI
     tile = (MODES, LANES)
     dma = pltpu.SemaphoreType.DMA
@@ -534,11 +575,21 @@
         functools.partial(kernel, gx_size, gy_size),
         out_shape=(
             jax.ShapeDtypeStruct((MODES * ROWS, LANES), F32),
-            jax.ShapeDtypeStruct((8, LANES), F32),
+            jax.ShapeDtypeStruct((4, MODES), F32),
         ),
-        in_specs=[vmem, vmem, smem, smem, vmem, vmem, vmem],
-        out_specs=(vmem, vmem),
+        in_specs=[hbm] * 7,
+        out_specs=(hbm, vmem),
         scratch_shapes=[
+            pltpu.VMEM((MODES * ROWS, LANES), F32),
+            pltpu.SemaphoreType.DMA,
+            pltpu.VMEM((MODES * ROWS, LANES), F32),
+            pltpu.VMEM((ROWS, LANES), I32),
+            pltpu.SMEM((LAYERS,), F32),
+            pltpu.SMEM((LAYERS, MODES - 1), F32),
+            pltpu.VMEM((MODES,) * 3, F32),
+            pltpu.VMEM((2, 1, NZ), I32),
+            pltpu.VMEM((net_place.shape[0] // LANES, LANES), I32),
+            pltpu.SemaphoreType.DMA((7,)),
             pltpu.VMEM((NZ, 2) + tile, F32),
             pltpu.VMEM((ROWS + 4,) + tile, F32),
             pltpu.VMEM((ROWS + 4,) + tile, F32),
@@ -548,8 +599,8 @@
             pltpu.VMEM((ROWS,) + tile, F32),
             pltpu.VMEM((ROWS,) + tile, F32),
             pltpu.VMEM((2, ROWS, LANES), I32),
-            pltpu.VMEM((8, LANES), I32),
-            pltpu.VMEM((8, 8, LANES), I32),
+            pltpu.VMEM((3, 1, LANES), I32),
+            pltpu.VMEM((8, 3, 1, LANES), I32),
             pltpu.VMEM(tile, F32),
             pltpu.VMEM((2,) + tile, F32),
             pltpu.VMEM((LAYERS * MODES, 3 * MODES), BF16),
@@ -567,7 +618,7 @@
             dma((g1,)), dma((g1,)), dma((m_count,)), dma((m_count,)),
         ],
         compiler_params=pltpu.CompilerParams(
-            collective_id=0, has_side_effects=True, vmem_limit_bytes=48 * 1024 * 1024
+            collective_id=0, has_side_effects=True, vmem_limit_bytes=67043328
         ),
     )(
         charge_density.reshape(MODES * ROWS, LANES),
@@ -575,12 +626,10 @@
         eps_mean,
         eps_fluct,
         galerkin,
-        net_ids.reshape(ROWS, 1),
+        jnp.transpose(net_ids, (1, 2, 0)),
         net_place.reshape(-1, LANES),
     )
-    mine = charges[:, :8].reshape(8, 2, 4)
-    charges = jnp.transpose(mine, (1, 0, 2)).reshape(MODES, 4)
-    return potential.reshape(charge_density.shape), charges
+    return potential.reshape(charge_density.shape), charges.T
 
 
 def solution(mesh):

time: 58.6 us -> 52.1 us (0.89)
  Pallas kernels: 52.7 us -> 48.8 us
  local copies, waits for them, and re-layouts: 4.94 us -> 2.47 us
    pallas_call x1, Pallas kernels: 52.7 us -> 48.8 us  [local(): pl.pallas_call(functools.partial(kernel, gx_size, gy_size), out_shape=(ja...]
    unnamed x16 -> x4, local copies, waits for them, and re-layouts: 4.13 us -> 2.47 us
    reshape x2 -> x0, local copies, waits for them, and re-layouts: 0.73 us -> none  [the longest x1 0.66 us: local(): charges = jnp.transpose(mine, (1, 0, 2)).reshape(MODES, 4)]
where the time goes in v2:
time: 52.1 us; the launch traced here: 51.9 us
  Pallas kernels  48.8 us (94%)
  local copies, waits for them, and re-layouts  2.47 us (5%)
  between operations  0.65 us (1%)
    pallas_call x1, Pallas kernels, local(): pl.pallas_call(functools.partial(kernel, gx_size, gy_size), out_shape=(ja...  48.8 us
    unnamed x4, local copies, waits for them, and re-layouts  2.47 us

profile of v2, /device:TPU:1, one launch (start us, length us, event | category | flops | bytes accessed | tf_op | source)
XLA Modules:
  0.0 51.9 jit_solution(2476637510052697595)
XLA Ops:
  0.6 48.8 %shard_map.86 = (f32[1024,128]{1,0:T(8,128)}, f32[4,16]{1,0:T(4,128)}) custom-call(f32[1024,128]{1,0:T(8,128)} %bitcast.6, s32[64,128]{1,0:T(8,128)} %bitcast.8, f32[8]{0:T(128)} %mean_hbm.1, f32[8,15]{1,0:T(8,128)} %fluct_hbm.1, f32[16,16,16]{2,1,0:T(8,128)} %g_hbm.1, s32[2,1,32]{2,1,0:T(1,128)} %bitcast.11, s32[16,128]{1,0:T(8,128)} %bitcast.9), custom_call_target="tpu_custom_call" | custom-call | tf_op jit(solution)/shard_map/pallas_call | solution.py:574
  49.5 0.0 copy-start
  49.5 1.9 %copy.11 = f32[16,32,2,128]{3,2,1,0:T(2,128)} copy(f32[16,32,2,128]{3,2,1,0:T(2,128)} %bitcast.7) | data formatting | bytes 1048576
  51.3 0.0 copy-done
  51.3 0.6 %copy.12 = f32[16,4]{0,1:T(4,128)} copy(f32[16,4]{0,1:T(4,128)S(1)} %bitcast.10) | data formatting | bytes 512
Async XLA Ops:
  49.5 1.9 %copy-start = (f32[4,16]{1,0:T(4,128)S(1)}, f32[4,16]{1,0:T(4,128)}, u32[]{:S(2)}) copy-start(f32[4,16]{1,0:T(4,128)} %get-tuple-element.5) | copy-start | bytes 772

commit v3 on v2

--- a/solution.py
+++ b/solution.py
@@ -14,7 +14,7 @@
 SX, Y_HI = 4, 2
 MODES, LAYERS = 16, 8
 NZ, ROWS, LANES = 32, 64, 128
-CHUNK = 8
+CHUNK = 32
 MESH = pl.DeviceIdType.MESH
 F32, BF16, I32 = jnp.float32, jnp.bfloat16, jnp.int32
 

time: 52.1 us -> 47.1 us (0.904)
  Pallas kernels: 48.8 us -> 43.9 us
    pallas_call x1, Pallas kernels: 48.8 us -> 43.9 us  [local(): pl.pallas_call(functools.partial(kernel, gx_size, gy_size), out_shape=(ja...]
where the time goes in v3:
time: 47.1 us; the launch traced here: 47 us
  Pallas kernels  43.9 us (93%)
  local copies, waits for them, and re-layouts  2.47 us (5%)
  between operations  0.65 us (1%)
    pallas_call x1, Pallas kernels, local(): pl.pallas_call(functools.partial(kernel, gx_size, gy_size), out_shape=(ja...  43.9 us
    unnamed x4, local copies, waits for them, and re-layouts  2.47 us

profile of v3, /device:TPU:1, one launch (start us, length us, event | category | flops | bytes accessed | tf_op | source)
XLA Modules:
  0.0 47.0 jit_solution(2410241955039913863)
XLA Ops:
  0.6 43.9 %shard_map.86 = (f32[1024,128]{1,0:T(8,128)}, f32[4,16]{1,0:T(4,128)}) custom-call(f32[1024,128]{1,0:T(8,128)} %bitcast.6, s32[64,128]{1,0:T(8,128)} %bitcast.8, f32[8]{0:T(128)} %mean_hbm.1, f32[8,15]{1,0:T(8,128)} %fluct_hbm.1, f32[16,16,16]{2,1,0:T(8,128)} %g_hbm.1, s32[2,1,32]{2,1,0:T(1,128)} %bitcast.11, s32[16,128]{1,0:T(8,128)} %bitcast.9), custom_call_target="tpu_custom_call" | custom-call | tf_op jit(solution)/shard_map/pallas_call | solution.py:574
  44.5 0.0 copy-start
  44.5 1.9 %copy.11 = f32[16,32,2,128]{3,2,1,0:T(2,128)} copy(f32[16,32,2,128]{3,2,1,0:T(2,128)} %bitcast.7) | data formatting | bytes 1048576
  46.4 0.0 copy-done
  46.4 0.6 %copy.12 = f32[16,4]{0,1:T(4,128)} copy(f32[16,4]{0,1:T(4,128)S(1)} %bitcast.10) | data formatting | bytes 512
Async XLA Ops:
  44.5 1.9 %copy-start = (f32[4,16]{1,0:T(4,128)S(1)}, f32[4,16]{1,0:T(4,128)}, u32[]{:S(2)}) copy-start(f32[4,16]{1,0:T(4,128)} %get-tuple-element.5) | copy-start | bytes 772

commit v4 on v3

--- a/solution.py
+++ b/solution.py
@@ -14,7 +14,7 @@
 SX, Y_HI = 4, 2
 MODES, LAYERS = 16, 8
 NZ, ROWS, LANES = 32, 64, 128
-CHUNK = 32
+CHUNK = 64
 MESH = pl.DeviceIdType.MESH
 F32, BF16, I32 = jnp.float32, jnp.bfloat16, jnp.int32
 
@@ -136,12 +136,10 @@
         def _(q=q):
             pl.semaphore_signal(barrier, inc=1, device_id=target(q), device_id_type=MESH)
 
-    @pl.loop(1, g1)
-    def _(s):
+    for s in range(1, g1):
         pl.semaphore_signal(barrier, inc=1, device_id=group_peer(s)[0], device_id_type=MESH)
 
-    @pl.loop(1, m_count)
-    def _(s):
+    for s in range(1, m_count):
         pl.semaphore_signal(barrier, inc=1, device_id=member_peer(s), device_id_type=MESH)
 
     lane16 = lanes((MODES, LANES))
@@ -524,8 +522,7 @@
             s2, r2.at[s], r2_s.at[s], r2_r.at[s], device_id=member_peer(s), device_id_type=MESH
         )
 
-    @pl.loop(1, g1)
-    def _(s):
+    for s in range(1, g1):
         r1_copy(s).start()
 
     @pl.loop(1, g1, init_carry=s1[group])
@@ -535,8 +532,7 @@
 
     s2[...] = share
 
-    @pl.loop(1, m_count)
-    def _(s):
+    for s in range(1, m_count):
         r2_copy(s).start()
 
     @pl.loop(1, m_count, init_carry=share)

time: 47.1 us -> 45.3 us (0.962)
  Pallas kernels: 43.9 us -> 42 us
    pallas_call x1, Pallas kernels: 43.9 us -> 42 us  [local(): pl.pallas_call(functools.partial(kernel, gx_size, gy_size), out_shape=(ja...]
where the time goes in v4:
time: 45.3 us; the launch traced here: 45.1 us
  Pallas kernels  42 us (93%)
  local copies, waits for them, and re-layouts  2.47 us (5%)
  between operations  0.65 us (1%)
    pallas_call x1, Pallas kernels, local(): pl.pallas_call(functools.partial(kernel, gx_size, gy_size), out_shape=(ja...  42 us
    unnamed x4, local copies, waits for them, and re-layouts  2.47 us

profile of v4, /device:TPU:1, one launch (start us, length us, event | category | flops | bytes accessed | tf_op | source)
XLA Modules:
  0.0 45.1 jit_solution(16480880442149397687)
XLA Ops:
  0.6 42.0 %shard_map.86 = (f32[1024,128]{1,0:T(8,128)}, f32[4,16]{1,0:T(4,128)}) custom-call(f32[1024,128]{1,0:T(8,128)} %bitcast.6, s32[64,128]{1,0:T(8,128)} %bitcast.8, f32[8]{0:T(128)} %mean_hbm.1, f32[8,15]{1,0:T(8,128)} %fluct_hbm.1, f32[16,16,16]{2,1,0:T(8,128)} %g_hbm.1, s32[2,1,32]{2,1,0:T(1,128)} %bitcast.11, s32[16,128]{1,0:T(8,128)} %bitcast.9), custom_call_target="tpu_custom_call" | custom-call | tf_op jit(solution)/shard_map/pallas_call | solution.py:570
  42.7 0.0 copy-start
  42.7 1.9 %copy.11 = f32[16,32,2,128]{3,2,1,0:T(2,128)} copy(f32[16,32,2,128]{3,2,1,0:T(2,128)} %bitcast.7) | data formatting | bytes 1048576
  44.6 0.0 copy-done
  44.6 0.6 %copy.12 = f32[16,4]{0,1:T(4,128)} copy(f32[16,4]{0,1:T(4,128)S(1)} %bitcast.10) | data formatting | bytes 512
Async XLA Ops:
  42.7 1.9 %copy-start = (f32[4,16]{1,0:T(4,128)S(1)}, f32[4,16]{1,0:T(4,128)}, u32[]{:S(2)}) copy-start(f32[4,16]{1,0:T(4,128)} %get-tuple-element.5) | copy-start | bytes 772

commit v5 on v4

--- a/solution.py
+++ b/solution.py
@@ -225,7 +225,7 @@
             found += [e_copy(q)]
         return found
 
-    for q in (4, 5, 6, 7, 2, 3, 0, 1):
+    for q in (2, 3, 0, 1, 4, 5, 6, 7):
         @pl.when(exists(q))
         def _(q=q):
             for one in copies(q):
@@ -377,13 +377,12 @@
     )
     spot_p = jnp.where(spot_m < m_count, spot_p, -2)
 
-    @pl.loop(0, g1 // 2)
-    def _(pair):
+    for pair in range(g1 // 2):
         base = (2 * pair // SX) * CORES * per_gx + ((2 * pair) % SX) * Y_HI * 4
         for b, column in enumerate(columns):
             hit = spot_p == column - base
             hit = jnp.logical_and(hit, spot_p >= 0)
-            oht[pl.ds(pl.multiple_of(pair * LANES, LANES), LANES), b * LANES : (b + 1) * LANES] = (
+            oht[pair * LANES : (pair + 1) * LANES, b * LANES : (b + 1) * LANES] = (
                 jnp.where(hit, 1.0, 0.0).astype(BF16)
             )
 

time: 45.3 us -> 45.1 us (level)
  no operation moved by 1% of the time
where the time goes in v5:
time: 45.1 us; the launch traced here: 44.9 us
  Pallas kernels  41.8 us (93%)
  local copies, waits for them, and re-layouts  2.47 us (5%)
  between operations  0.65 us (1%)
    pallas_call x1, Pallas kernels, local(): pl.pallas_call(functools.partial(kernel, gx_size, gy_size), out_shape=(ja...  41.8 us
    unnamed x4, local copies, waits for them, and re-layouts  2.47 us

profile of v5, /device:TPU:1, one launch (start us, length us, event | category | flops | bytes accessed | tf_op | source)
XLA Modules:
  0.0 44.9 jit_solution(13245220813197254345)
XLA Ops:
  0.6 41.8 %shard_map.86 = (f32[1024,128]{1,0:T(8,128)}, f32[4,16]{1,0:T(4,128)}) custom-call(f32[1024,128]{1,0:T(8,128)} %bitcast.6, s32[64,128]{1,0:T(8,128)} %bitcast.8, f32[8]{0:T(128)} %mean_hbm.1, f32[8,15]{1,0:T(8,128)} %fluct_hbm.1, f32[16,16,16]{2,1,0:T(8,128)} %g_hbm.1, s32[2,1,32]{2,1,0:T(1,128)} %bitcast.11, s32[16,128]{1,0:T(8,128)} %bitcast.9), custom_call_target="tpu_custom_call" | custom-call | tf_op jit(solution)/shard_map/pallas_call | solution.py:569
  42.5 0.0 copy-start
  42.5 1.9 %copy.11 = f32[16,32,2,128]{3,2,1,0:T(2,128)} copy(f32[16,32,2,128]{3,2,1,0:T(2,128)} %bitcast.7) | data formatting | bytes 1048576
  44.3 0.0 copy-done
  44.4 0.6 %copy.12 = f32[16,4]{0,1:T(4,128)} copy(f32[16,4]{0,1:T(4,128)S(1)} %bitcast.10) | data formatting | bytes 512
Async XLA Ops:
  42.5 1.9 %copy-start = (f32[4,16]{1,0:T(4,128)S(1)}, f32[4,16]{1,0:T(4,128)}, u32[]{:S(2)}) copy-start(f32[4,16]{1,0:T(4,128)} %get-tuple-element.5) | copy-start | bytes 772
